TPU v7x, 32 devices: a whole 2x2x4 slice. The times are simulated.
32 devices in a mesh: groups: 2 (over x), blk: 8 (over z, y), sub: 2 (over core).
Axes of the slice: x: 2, y: 2, z: 4, core: 2. Of those that a mesh axis runs over, the one named last changes fastest.
Arguments:
- embeddings: bfloat16 [6144, 1024], P(('groups', 'blk', 'sub')), parts along dimension 0, may hold values from -6 to 6
- member_key: int32 [6144], P(('groups', 'blk', 'sub')), parts along dimension 0, may hold values from 0 to 1073741823, as said below
- limit_index: int32 [2], P('groups'), parts along dimension 0, may hold values from 0 to 7
Outputs:
- max_cosine: float32 [6144], P(('groups', 'blk', 'sub')), parts along dimension 0
- kept_share: float32 [2], P('groups'), parts along dimension 0
There are 2 independent parts, one for each index of `groups`. A program takes and returns all parts, laid end to end along the dimension named above; each array names one. Nothing has to cross between parts.
Inputs may be any that keep to these rules, and one draw needn't show every extreme that they name: `member_key`: all keys of a cluster are distinct. A key's quotient by 268435456 is the member's sub-cluster, 0 to 3; its remainder orders the members.
All inputs are finite; a program needn't handle non-finite values.
Results may differ from a plain program's by a relative error of at most 0.0013.
Values may be sent and summed in bfloat16 or wider, within the bound.
A program may use at most 64 MiB of HBM per device.

v0:
```python
import math

import jax
import jax.numpy as jnp
from jax import lax
from jax.sharding import PartitionSpec as P

LIMITS = 8


label_stride = 268435456


def normalize(embeddings):
    values = embeddings.astype(jnp.float32)
    mean_square = jnp.mean(values * values, axis=1, keepdims=True)
    scaled = values * lax.rsqrt(mean_square + 1e-06) * (1.0 / math.sqrt(values.shape[1]))
    return scaled.astype(jnp.bfloat16)


def make_absorb(rows, row_key, key_seen):
    row_label = row_key // label_stride

    def absorb(best, piece, start):
        other_label = key_seen // label_stride
        scores = lax.dot_general(
            rows, piece, (((1,), (1,)), ((), ())), preferred_element_type=jnp.float32
        )
        allowed = (key_seen[None, :] < row_key[:, None]) & (
            other_label[None, :] == row_label[:, None]
        )
        return jnp.maximum(best, jnp.max(jnp.where(allowed, scores, jnp.float32(-1.0)), axis=1))

    return absorb


def on_device(embeddings, member_key, limit_index):
    unit = normalize(embeddings)
    own_rows = unit.shape[0]
    key_all = lax.all_gather(member_key, ("blk", "sub"), axis=0, tiled=True)
    absorb = make_absorb(unit, member_key, key_all)
    start_best = jnp.full((own_rows,), -1.0, jnp.float32)
    max_cosine = absorb(
        start_best, lax.all_gather(unit, ("blk", "sub"), axis=0, tiled=True), jnp.int32(0)
    )
    width = math.sqrt(unit.shape[1])
    table = (2.0 + 0.5 * jnp.arange(LIMITS, dtype=jnp.float32)) / width
    limit = jnp.sum(
        jnp.where(jnp.arange(LIMITS, dtype=jnp.int32) == limit_index[0], table, jnp.float32(0.0))
    )
    kept = jax.nn.sigmoid(2.0 * width * (limit - max_cosine))
    kept_sum = lax.psum(jnp.sum(kept), ("blk", "sub"))
    kept_share = (kept_sum / key_all.shape[0]).reshape(1)
    return (max_cosine, kept_share)


def solution(mesh):
    in_specs = (P(("groups", "blk", "sub"), None), P(("groups", "blk", "sub")), P("groups"))
    out_specs = (P(("groups", "blk", "sub")), P("groups"))
    return jax.shard_map(
        on_device, mesh=mesh, in_specs=in_specs, out_specs=out_specs, check_vma=False
    )
```

profile of v0, /device:TPU:0, one launch (start us, length us, event | category | flops | bytes accessed | tf_op | source)
XLA Modules:
  0.0 126.1 jit_solution(16782089662486154590)
XLA Ops:
  7.2 0.0 all-gather.2.cloned.1.call-start
  7.2 1.2 fusion.1
  8.4 1.9 %fusion.3 = bf16[192,1024]{1,0:T(8,128)(2,1)} fusion(bf16[192,1024]{1,0:T(8,128)(2,1)} %param.3, f32[192]{0:T(256)S(1)} %add_rsqrt_fusion), kind=kLoop, calls=%fused_computation.6 | loop fusion | flops 786432 | bytes 787200 | tf_op jit(solution)/shard_map/convert_element_type | solution.py:18
  10.3 0.0 all-gather.2.cloned.1.call-update
  11.0 1.2 dynamic-slice
  12.9 0.9 dynamic-update-slice
  13.8 0.7 fusion.7
  14.5 65.1 %all-reduce = s32[3072]{0:T(1024)S(1)} all-reduce(s32[3072]{0:T(1024)S(1)} %dynamic-update-slice), channel_id=1, replica_groups=mesh['groups'=2,'blk'=8,'sub'=2] {'blk','sub'}, use_global_device_ids=true, to_apply=%add | all-reduce | flops 3072 | bytes 24576
  79.6 0.7 and_select_fusion
  80.3 0.0 all-gather.2.cloned.1.call-done
  80.3 5.2 %fusion = f32[192]{0:T(256)S(1)} fusion(bf16[192,1024]{1,0:T(8,128)(2,1)} %fusion.3, bf16[3072,1024]{1,0:T(8,128)(2,1)} %all-gather.2.cloned.1.call-done, s32[3072]{0:T(1024)S(1)} %add_select_fusion, s32[3072]{0:T(1024)S(1)} %all-reduce, s32[192]{0:T(256)S(1)} %and_select_fusion, s32[192]{0:T(256)} %param.4), kind=kOutput, calls=%fused_computation.1 | convolution fusion | flops 1210908416 | bytes 6711552 | tf_op jit(solution)/shard_map/dot_general | solution.py:26
  85.5 1.9 %fusion.6 = (f32[]{:T(128)}, f32[192]{0:T(256)}) fusion(f32[]{:T(128)} %fusion.7, f32[192]{0:T(256)S(1)} %fusion), kind=kLoop, calls=%fused_computation.21 | loop fusion | flops 1343 | bytes 1544 | tf_op jit(solution)/shard_map/reduce_sum | solution.py:52
  87.4 30.1 %psum.7 = f32[]{:T(128)} all-reduce(f32[]{:T(128)} %get-tuple-element.2), channel_id=1, replica_groups=mesh['groups'=2,'blk'=8,'sub'=2] {'blk','sub'}, use_global_device_ids=true, to_apply=%region_4.5 | all-reduce | flops 1 | bytes 8 | tf_op jit(solution)/shard_map/psum | solution.py:52
  (3 shorter events, 0.0 us)
Async XLA Ops:
  7.2 73.1 %all-gather.2.cloned.1.call-start = ((), (), s32[]{:S(2)}) async-start(), calls=%async_computation | async-start | bytes 6684672 | tf_op jit(solution)/shard_map/all_gather | solution.py:44
Sparse Core Ops, SparseCore 0:
  10.5 64.6 all-gather.1
where the time goes:
time: 126 us
  blocking collectives  95.2 us (76%)
  between operations  17.1 us (14%)
  other arithmetic  6.33 us (5%)
  matrix products  5.23 us (4%)
  local copies, waits for them, and re-layouts  2.14 us (2%)
    unnamed x1, blocking collectives  65.1 us
    psum x1, blocking collectives, on_device(): kept_sum = lax.psum(jnp.sum(kept), ('blk', 'sub'))  30.1 us
    dot_general x1, matrix products, absorb(): lax.dot_general(rows, piece, (((1,), (1,)), ((), ())), preferred_element_...  5.23 us
  transfers between devices with their start and end apart: 1, of which 0 were waited for; matrix products, arithmetic and copies ran while one was open for 3% of the time, Pallas kernels for 0%

commit v1 on v0

v1 whole, which is shorter than its diff:
```python
import functools
import math

import jax
import jax.numpy as jnp
from jax import lax
from jax.experimental import pallas as pl
from jax.experimental.pallas import tpu as pltpu
from jax.sharding import PartitionSpec as P

MESH = pl.DeviceIdType.MESH
LANES = 128
label_stride = 268435456


def normalize(block):
    values = block.astype(jnp.float32)
    mean_square = jnp.mean(values * values, axis=1, keepdims=True)
    scaled = values * lax.rsqrt(mean_square + 1e-06) * (1.0 / math.sqrt(values.shape[1]))
    return scaled.astype(jnp.bfloat16)


def ring_place(index, n):
    odd = lax.rem(index, 2)
    return (1 - odd) * lax.div(index, 2) + odd * (n - 1 - lax.div(index, 2))


def ring_index(place, n):
    late = lax.div(place, n // 2)
    return (1 - late) * (2 * place) + late * (2 * (n - 1 - place) + 1)


def kernel(
    n, subs, reach, chunks,
    x_hbm, key_ref, limit_ref, best_ref, share_ref,
    left, right, unit_left, unit_right, keys,
    row_out, row_in, col_out, col_in, sums,
    load_sem, key_send, key_recv,
    up_send, up_recv, down_send, down_recv, side_send, side_recv,
    row_send, row_recv, col_send, col_recv, sum_send, sum_recv,
):
    rows, width = x_hbm.shape
    piece = rows // chunks
    blk = lax.axis_index("blk")
    sub = lax.axis_index("sub")
    place = ring_place(blk, n)

    def device(offset, sub_step):
        there = ring_index(lax.rem(place + offset + n, n), n)
        return {"blk": there, "sub": lax.rem(sub + sub_step, subs)}

    def remote(src, dst, send, recv, offset, sub_step):
        return pltpu.make_async_remote_copy(
            src_ref=src, dst_ref=dst, send_sem=send, recv_sem=recv,
            device_id=device(offset, sub_step), device_id_type=MESH,
        )

    load = pltpu.make_async_copy(x_hbm, right.at[0, sub], load_sem)
    load.start()

    others = [(o, s) for o in range(n) for s in range(subs) if (o, s) != (0, 0)]
    barrier = pltpu.get_barrier_semaphore()
    for o, s in others:
        pl.semaphore_signal(barrier, inc=1, device_id=device(o, s), device_id_type=MESH)
    keys[reach, sub] = key_ref[...]
    pl.semaphore_wait(barrier, len(others))

    load.wait()
    span = lambda k: pl.ds(k * piece, piece)
    up, down, side = {}, {}, {}
    for hop in range(1, reach + 1):
        for k in range(chunks):
            src = right.at[0, sub, span(k)] if hop == 1 else left.at[hop - 2, span(k)]
            up[hop, k] = remote(
                src, left.at[hop - 1, span(k)], up_send.at[hop - 1, k], up_recv.at[hop - 1, k], 1, 0
            )
            down[hop, k] = remote(
                right.at[hop - 1, sub, span(k)], right.at[hop, sub, span(k)],
                down_send.at[hop - 1, k], down_recv.at[hop - 1, k], -1, 0,
            )
    for hop in range(reach + 1):
        for k in range(chunks):
            for s in range(1, subs):
                here = right.at[hop, sub, span(k)]
                side[hop, k, s] = remote(
                    here, here, side_send.at[hop, k, s - 1], side_recv.at[hop, k, s - 1], 0, s
                )
    key_copies = [
        remote(
            key_ref, keys.at[reach - o, sub],
            key_send.at[reach - o, s], key_recv.at[reach - o, s], o, s,
        )
        for o in range(-reach, reach + 1) for s in range(subs) if (o, s) != (0, 0)
    ]

    for k in range(chunks):
        up[1, k].start()
        down[1, k].start()
    for k in range(chunks):
        for s in range(1, subs):
            side[0, k, s].start()
    for copy in key_copies:
        copy.start()

    unit_right[0, sub] = normalize(right[0, sub])
    for k in range(chunks):
        for s in range(1, subs):
            side[0, k, s].wait_recv()
    for s in range(1, subs):
        unit_right[0, lax.rem(sub + s, subs)] = normalize(right[0, lax.rem(sub + s, subs)])
    for copy in key_copies:
        copy.wait_recv()

    floor = jnp.float32(-1.0)
    wide = subs * rows
    best_row, best_col = {}, {}

    def compare(back, ahead):
        lhs = unit_right[0, sub] if back == 0 else unit_left[back - 1]
        rhs = unit_right[ahead].reshape(wide, width)
        scores = lax.dot_general(
            lhs, rhs, (((1,), (1,)), ((), ())), preferred_element_type=jnp.float32
        )
        row_key = jnp.broadcast_to(keys[reach - back, sub], (LANES, rows)).T
        col_key = jnp.concatenate([keys[reach + ahead, s] for s in range(subs)], axis=1)
        columns = []
        for start in range(0, wide, LANES):
            tile = scores[:, start : start + LANES]
            other = jnp.broadcast_to(col_key[:, start : start + LANES], (rows, LANES))
            same = jnp.where((row_key ^ other) < label_stride, tile, floor)
            earlier = other < row_key
            to_row = jnp.where(earlier, same, floor)
            best_row[back] = jnp.maximum(best_row[back], to_row) if back in best_row else to_row
            if ahead or back:
                columns.append(jnp.max(jnp.where(earlier, floor, same), axis=0, keepdims=True))
        if columns:
            column = jnp.concatenate(columns, axis=1)
            best_col[ahead] = (
                jnp.maximum(best_col[ahead], column) if ahead in best_col else column
            )

    def row_of(back):
        return jnp.max(best_row[back].T, axis=0, keepdims=True)

    pairs = [(d // 2, d - d // 2) for d in range(min(2 * reach, n // 2) + 1)]
    last_row = {b: max(i for i, p in enumerate(pairs) if p[0] == b) for b in {p[0] for p in pairs}}
    last_col = {a: max(i for i, p in enumerate(pairs) if p[1] == a) for a in {p[1] for p in pairs}}
    row_copies, col_copies = [], []

    def run(i):
        back, ahead = pairs[i]
        compare(back, ahead)
        if back and last_row[back] == i:
            row_out[back - 1] = row_of(back)
            copy = remote(
                row_out.at[back - 1], row_in.at[back - 1],
                row_send.at[back - 1], row_recv.at[back - 1], -back, 0,
            )
            copy.start()
            row_copies.append(copy)
        if ahead and last_col[ahead] == i:
            for s in range(subs):
                col_out[ahead - 1, s] = best_col[ahead][:, s * rows : (s + 1) * rows]
            for s in range(subs):
                target = lax.rem(sub + s, subs)
                copy = remote(
                    col_out.at[ahead - 1, target], col_in.at[ahead - 1, sub],
                    col_send.at[ahead - 1, s], col_recv.at[ahead - 1, s], ahead, s,
                )
                copy.start()
                col_copies.append(copy)

    run(0)
    done = 1
    for hop in range(1, reach + 1):
        for k in range(chunks):
            up[hop, k].wait_recv()
            if hop < reach:
                up[hop + 1, k].start()
            down[hop, k].wait_recv()
            if hop < reach:
                down[hop + 1, k].start()
            for s in range(1, subs):
                side[hop, k, s].start()
            unit_left[hop - 1, span(k)] = normalize(left[hop - 1, span(k)])
            unit_right[hop, sub, span(k)] = normalize(right[hop, sub, span(k)])
            for s in range(1, subs):
                side[hop, k, s].wait_recv()
                there = lax.rem(sub + s, subs)
                unit_right[hop, there, span(k)] = normalize(right[hop, there, span(k)])
        while done < len(pairs) and max(pairs[done]) <= hop:
            run(done)
            done += 1

    for copy in row_copies + col_copies:
        copy.wait_recv()
    best = jnp.maximum(row_of(0), floor)
    for back in last_row:
        if back:
            best = jnp.maximum(best, row_in[back - 1])
    for ahead in last_col:
        if ahead:
            for s in range(subs):
                best = jnp.maximum(best, col_in[ahead - 1, s])
    best_ref[...] = best

    scale = math.sqrt(width)
    limit = (2.0 + 0.5 * jnp.full((1, rows), limit_ref[0], jnp.int32).astype(jnp.float32)) / scale
    kept = jax.nn.sigmoid(2.0 * scale * (limit - best))
    total = jnp.sum(kept, axis=1, keepdims=True)
    sums[blk, sub] = jnp.broadcast_to(total, (1, LANES))
    sum_copies = [
        remote(
            sums.at[blk, sub], sums.at[blk, sub],
            sum_send.at[o, s], sum_recv.at[o, s], o, s,
        )
        for o, s in others
    ]
    for copy in sum_copies:
        copy.start()
    for copies in (up, down, side):
        for copy in copies.values():
            copy.wait_send()
    for copy in key_copies + row_copies + col_copies:
        copy.wait_send()
    for copy in sum_copies:
        copy.wait_recv()
    everything = jnp.sum(sums[...].reshape(n * subs, LANES), axis=0, keepdims=True)
    share_ref[...] = (everything / (n * subs * rows))[:, :1]
    for copy in sum_copies:
        copy.wait_send()


def solution(mesh):
    n, subs = mesh.shape["blk"], mesh.shape["sub"]

    def on_device(embeddings, member_key, limit_index):
        rows, width = embeddings.shape
        reach = -(-(n // 2) // 2)
        chunks = 4 if rows % 64 == 0 else 1
        dma = pltpu.SemaphoreType.DMA
        raw, f32, i32 = embeddings.dtype, jnp.float32, jnp.int32
        held = (2 * reach + 1 + (2 * reach + 2) * (subs - 1)) * 2
        best, share = pl.pallas_call(
            functools.partial(kernel, n, subs, reach, chunks),
            out_shape=(
                jax.ShapeDtypeStruct((1, rows), f32),
                jax.ShapeDtypeStruct((1, 1), f32),
            ),
            in_specs=[
                pl.BlockSpec(memory_space=pl.ANY),
                pl.BlockSpec(memory_space=pltpu.VMEM),
                pl.BlockSpec(memory_space=pltpu.SMEM),
            ],
            out_specs=(
                pl.BlockSpec(memory_space=pltpu.VMEM),
                pl.BlockSpec(memory_space=pltpu.VMEM),
            ),
            scratch_shapes=[
                pltpu.VMEM((reach, rows, width), raw),
                pltpu.VMEM((reach + 1, subs, rows, width), raw),
                pltpu.VMEM((reach, rows, width), jnp.bfloat16),
                pltpu.VMEM((reach + 1, subs, rows, width), jnp.bfloat16),
                pltpu.VMEM((2 * reach + 1, subs, 1, rows), i32),
                pltpu.VMEM((reach, 1, rows), f32),
                pltpu.VMEM((reach, 1, rows), f32),
                pltpu.VMEM((reach, subs, 1, rows), f32),
                pltpu.VMEM((reach, subs, 1, rows), f32),
                pltpu.VMEM((n, subs, 1, LANES), f32),
                dma,
                dma((2 * reach + 1, subs)),
                dma((2 * reach + 1, subs)),
                dma((reach, chunks)),
                dma((reach, chunks)),
                dma((reach, chunks)),
                dma((reach, chunks)),
                dma((reach + 1, chunks, max(subs - 1, 1))),
                dma((reach + 1, chunks, max(subs - 1, 1))),
                dma((reach,)),
                dma((reach,)),
                dma((reach, subs)),
                dma((reach, subs)),
                dma((n, subs)),
                dma((n, subs)),
            ],
            compiler_params=pltpu.CompilerParams(
                collective_id=0,
                has_side_effects=True,
                vmem_limit_bytes=held * rows * width * 2 + 16 * 2**20,
            ),
        )(embeddings, member_key.reshape(1, rows), limit_index)
        return best.reshape(rows), share.reshape(1)

    in_specs = (P(("groups", "blk", "sub"), None), P(("groups", "blk", "sub")), P("groups"))
    out_specs = (P(("groups", "blk", "sub")), P("groups"))
    return jax.shard_map(
        on_device, mesh=mesh, in_specs=in_specs, out_specs=out_specs, check_vma=False
    )
```

time: 126 us -> 44 us (0.35)
  blocking collectives: 95.2 us -> 0 us
  Pallas kernels: 0 us -> 38.5 us
  between operations: 17.1 us -> 3.06 us
  other arithmetic: 6.33 us -> 0 us
  matrix products: 5.23 us -> 0 us
    unnamed x1 -> x0, blocking collectives: 65.1 us -> none
    pallas_call x0 -> x1, Pallas kernels: none -> 38.5 us  [on_device(): pl.pallas_call(functools.partial(kernel, n, subs, reach, chunks), out_sha...]
    psum x1 -> x0, blocking collectives: 30.1 us -> none  [on_device(): kept_sum = lax.psum(jnp.sum(kept), ('blk', 'sub'))]
    dot_general x1 -> x0, matrix products: 5.23 us -> none  [absorb(): lax.dot_general(rows, piece, (((1,), (1,)), ((), ())), preferred_element_...]
    reduce_sum x3 -> x0, other arithmetic: 3.69 us -> none  [the longest x1 1.85 us: on_device(): kept_sum = lax.psum(jnp.sum(kept), ('blk', 'sub'))]
    convert_element_type x1 -> x0, other arithmetic: 1.93 us -> none  [normalize(): return scaled.astype(jnp.bfloat16)]
  transfers between devices with their start and end apart: 1 -> 0, of which waited for: 0 -> 0; matrix products, arithmetic and copies ran while one was open for 3% -> 0% of each run, Pallas kernels for 0% -> 0%
where the time goes in v1:
time: 44 us; the launch traced here: 43.8 us
  Pallas kernels  38.5 us (88%)
  between operations  3.06 us (7%)
  local copies, waits for them, and re-layouts  2.23 us (5%)
    pallas_call x1, Pallas kernels, on_device(): pl.pallas_call(functools.partial(kernel, n, subs, reach, chunks), out_sha...  38.5 us
    unnamed x5, local copies, waits for them, and re-layouts  2.23 us

profile of v1, /device:TPU:0, one launch (start us, length us, event | category | flops | bytes accessed | tf_op | source)
XLA Modules:
  0.0 43.8 jit_solution(18156122531529465187)
XLA Ops:
  1.3 0.0 copy-start.1
  1.3 0.7 %copy-done.1 = s32[192]{0:T(256)S(1)} copy-done((s32[192]{0:T(256)S(1)}, s32[192]{0:T(256)}, u32[]{:S(2)}) %copy-start.1) | copy-done | bytes 792
  2.0 0.0 copy-start
  2.0 1.0 %copy-done = bf16[192,1024]{1,0:T(8,128)(2,1)S(1)} copy-done((bf16[192,1024]{1,0:T(8,128)(2,1)S(1)}, bf16[192,1024]{1,0:T(8,128)(2,1)}, u32[]{:S(2)}) %copy-start) | copy-done | bytes 393240
  3.0 38.5 %shard_map.50 = (f32[1,192]{1,0:T(1,128)S(1)}, f32[1,1]{1,0:T(1,128)}) custom-call(bf16[192,1024]{1,0:T(8,128)(2,1)S(1)} %copy-done, s32[1,192]{1,0:T(1,128)S(1)} %bitcast.3, s32[1]{0:T(128)S(6)} %copy.7.limit_ref), custom_call_target="tpu_custom_call" | custom-call | tf_op jit(solution)/shard_map/pallas_call | solution.py:244
  41.5 0.6 %copy.8 = f32[192]{0:T(256)} copy(f32[192]{0:T(256)S(1)} %bitcast.4) | data formatting | bytes 1536
Async XLA Ops:
  1.3 0.7 %copy-start.1 = (s32[192]{0:T(256)S(1)}, s32[192]{0:T(256)}, u32[]{:S(2)}) copy-start(s32[192]{0:T(256)} %param.4) | copy-start | bytes 2308
  2.0 1.0 %copy-start = (bf16[192,1024]{1,0:T(8,128)(2,1)S(1)}, bf16[192,1024]{1,0:T(8,128)(2,1)}, u32[]{:S(2)}) copy-start(bf16[192,1024]{1,0:T(8,128)(2,1)} %x_hbm.1) | copy-start | bytes 1179652

commit v2 on v1

--- a/solution.py
+++ b/solution.py
@@ -32,7 +32,7 @@
 
 def kernel(
     n, subs, reach, chunks,
-    x_hbm, key_ref, limit_ref, best_ref, share_ref,
+    x_hbm, key_hbm, limit_ref, best_ref, share_ref,
     left, right, unit_left, unit_right, keys,
     row_out, row_in, col_out, col_in, sums,
     load_sem, key_send, key_recv,
@@ -55,17 +55,20 @@
             device_id=device(offset, sub_step), device_id_type=MESH,
         )
 
-    load = pltpu.make_async_copy(x_hbm, right.at[0, sub], load_sem)
+    load = pltpu.make_async_copy(x_hbm, right.at[0, sub], load_sem.at[0])
     load.start()
+    load_key = pltpu.make_async_copy(key_hbm, keys.at[reach, sub], load_sem.at[1])
+    load_key.start()
 
     others = [(o, s) for o in range(n) for s in range(subs) if (o, s) != (0, 0)]
+    near = [(1, 0), (-1, 0)] + [(0, s) for s in range(1, subs)]
     barrier = pltpu.get_barrier_semaphore()
-    for o, s in others:
+    for o, s in near:
         pl.semaphore_signal(barrier, inc=1, device_id=device(o, s), device_id_type=MESH)
-    keys[reach, sub] = key_ref[...]
-    pl.semaphore_wait(barrier, len(others))
+    pl.semaphore_wait(barrier, len(near))
 
     load.wait()
+    load_key.wait()
     span = lambda k: pl.ds(k * piece, piece)
     up, down, side = {}, {}, {}
     for hop in range(1, reach + 1):
@@ -85,22 +88,30 @@
                 side[hop, k, s] = remote(
                     here, here, side_send.at[hop, k, s - 1], side_recv.at[hop, k, s - 1], 0, s
                 )
-    key_copies = [
-        remote(
-            key_ref, keys.at[reach - o, sub],
-            key_send.at[reach - o, s], key_recv.at[reach - o, s], o, s,
-        )
-        for o in range(-reach, reach + 1) for s in range(subs) if (o, s) != (0, 0)
-    ]
-
+    key_up, key_down, key_side = {}, {}, {}
+    for hop in range(1, reach + 1):
+        for table, way in ((key_up, -1), (key_down, 1)):
+            table[hop] = remote(
+                keys.at[reach + way * (hop - 1), sub], keys.at[reach + way * hop, sub],
+                key_send.at[reach + way * hop, 0], key_recv.at[reach + way * hop, 0], -way, 0,
+            )
+    for hop in range(reach + 1):
+        for s in range(1, subs):
+            here = keys.at[reach + hop, sub]
+            key_side[hop, s] = remote(
+                here, here, key_send.at[reach + hop, s], key_recv.at[reach + hop, s], 0, s
+            )
+
+    key_up[1].start()
+    key_down[1].start()
     for k in range(chunks):
         up[1, k].start()
         down[1, k].start()
     for k in range(chunks):
         for s in range(1, subs):
             side[0, k, s].start()
-    for copy in key_copies:
-        copy.start()
+    for s in range(1, subs):
+        key_side[0, s].start()
 
     unit_right[0, sub] = normalize(right[0, sub])
     for k in range(chunks):
@@ -108,8 +119,7 @@
             side[0, k, s].wait_recv()
     for s in range(1, subs):
         unit_right[0, lax.rem(sub + s, subs)] = normalize(right[0, lax.rem(sub + s, subs)])
-    for copy in key_copies:
-        copy.wait_recv()
+        key_side[0, s].wait_recv()
 
     floor = jnp.float32(-1.0)
     wide = subs * rows
@@ -173,6 +183,13 @@
     run(0)
     done = 1
     for hop in range(1, reach + 1):
+        key_up[hop].wait_recv()
+        key_down[hop].wait_recv()
+        if hop < reach:
+            key_up[hop + 1].start()
+            key_down[hop + 1].start()
+        for s in range(1, subs):
+            key_side[hop, s].start()
         for k in range(chunks):
             up[hop, k].wait_recv()
             if hop < reach:
@@ -188,6 +205,8 @@
                 side[hop, k, s].wait_recv()
                 there = lax.rem(sub + s, subs)
                 unit_right[hop, there, span(k)] = normalize(right[hop, there, span(k)])
+        for s in range(1, subs):
+            key_side[hop, s].wait_recv()
         while done < len(pairs) and max(pairs[done]) <= hop:
             run(done)
             done += 1
@@ -218,10 +237,10 @@
     ]
     for copy in sum_copies:
         copy.start()
-    for copies in (up, down, side):
+    for copies in (up, down, side, key_up, key_down, key_side):
         for copy in copies.values():
             copy.wait_send()
-    for copy in key_copies + row_copies + col_copies:
+    for copy in row_copies + col_copies:
         copy.wait_send()
     for copy in sum_copies:
         copy.wait_recv()
@@ -240,7 +259,6 @@
         chunks = 4 if rows % 64 == 0 else 1
         dma = pltpu.SemaphoreType.DMA
         raw, f32, i32 = embeddings.dtype, jnp.float32, jnp.int32
-        held = (2 * reach + 1 + (2 * reach + 2) * (subs - 1)) * 2
         best, share = pl.pallas_call(
             functools.partial(kernel, n, subs, reach, chunks),
             out_shape=(
@@ -248,8 +266,8 @@
                 jax.ShapeDtypeStruct((1, 1), f32),
             ),
             in_specs=[
-                pl.BlockSpec(memory_space=pl.ANY),
-                pl.BlockSpec(memory_space=pltpu.VMEM),
+                pl.BlockSpec(memory_space=pltpu.HBM),
+                pl.BlockSpec(memory_space=pltpu.HBM),
                 pl.BlockSpec(memory_space=pltpu.SMEM),
             ],
             out_specs=(
@@ -267,7 +285,7 @@
                 pltpu.VMEM((reach, subs, 1, rows), f32),
                 pltpu.VMEM((reach, subs, 1, rows), f32),
                 pltpu.VMEM((n, subs, 1, LANES), f32),
-                dma,
+                dma((2,)),
                 dma((2 * reach + 1, subs)),
                 dma((2 * reach + 1, subs)),
                 dma((reach, chunks)),
@@ -286,7 +304,6 @@
             compiler_params=pltpu.CompilerParams(
                 collective_id=0,
                 has_side_effects=True,
-                vmem_limit_bytes=held * rows * width * 2 + 16 * 2**20,
             ),
         )(embeddings, member_key.reshape(1, rows), limit_index)
         return best.reshape(rows), share.reshape(1)

time: 44 us -> 38.8 us (0.88)
  Pallas kernels: 38.5 us -> 34.4 us
  local copies, waits for them, and re-layouts: 2.23 us -> 1.21 us
    pallas_call x1, Pallas kernels: 38.5 us -> 34.4 us  [on_device(): pl.pallas_call(functools.partial(kernel, n, subs, reach, chunks), out_sha...]
    unnamed x5 -> x3, local copies, waits for them, and re-layouts: 2.23 us -> 1.21 us
where the time goes in v2:
time: 38.8 us; the launch traced here: 38.6 us
  Pallas kernels  34.4 us (89%)
  between operations  3.05 us (8%)
  local copies, waits for them, and re-layouts  1.21 us (3%)
    pallas_call x1, Pallas kernels, on_device(): pl.pallas_call(functools.partial(kernel, n, subs, reach, chunks), out_sha...  34.4 us
    unnamed x3, local copies, waits for them, and re-layouts  1.21 us

profile of v2, /device:TPU:0, one launch (start us, length us, event | category | flops | bytes accessed | tf_op | source)
XLA Modules:
  0.0 38.6 jit_solution(15157446485908675271)
XLA Ops:
  1.3 34.4 %shard_map.50 = (f32[1,192]{1,0:T(1,128)}, f32[1,1]{1,0:T(1,128)}) custom-call(bf16[192,1024]{1,0:T(8,128)(2,1)} %x_hbm.1, s32[1,192]{1,0:T(1,128)} %bitcast.3, s32[1]{0:T(128)S(6)} %copy.7.limit_ref), custom_call_target="tpu_custom_call" | custom-call | tf_op jit(solution)/shard_map/pallas_call | solution.py:262
  35.7 0.0 copy-start
  35.7 0.6 %copy-done = f32[1,192]{1,0:T(1,128)S(1)} copy-done((f32[1,192]{1,0:T(1,128)S(1)}, f32[1,192]{1,0:T(1,128)}, u32[]{:S(2)}) %copy-start) | copy-done | bytes 792
  36.3 0.6 %copy.8 = f32[192]{0:T(256)} copy(f32[192]{0:T(256)S(1)} %bitcast.4) | data formatting | bytes 1536
Async XLA Ops:
  35.7 0.7 %copy-start = (f32[1,192]{1,0:T(1,128)S(1)}, f32[1,192]{1,0:T(1,128)}, u32[]{:S(2)}) copy-start(f32[1,192]{1,0:T(1,128)} %get-tuple-element.4) | copy-start | bytes 2308

commit v3 on v2

--- a/solution.py
+++ b/solution.py
@@ -30,11 +30,18 @@
     return (1 - late) * (2 * place) + late * (2 * (n - 1 - place) + 1)
 
 
+def plan(n, reach):
+    pairs = [(d // 2, d - d // 2) for d in range(min(2 * reach, n // 2) + 1)]
+    last = [{p[side]: i for i, p in enumerate(pairs)} for side in (0, 1)]
+    late = [[v for v, i in table.items() if v and max(pairs[i]) == reach] for table in last]
+    return pairs, last[0], last[1], late[0], late[1]
+
+
 def kernel(
     n, subs, reach, chunks,
     x_hbm, key_hbm, limit_ref, best_ref, share_ref,
     left, right, unit_left, unit_right, keys,
-    row_out, row_in, col_out, col_in, sums,
+    row_out, row_in, col_out, col_in, table, maxima, ready,
     load_sem, key_send, key_recv,
     up_send, up_recv, down_send, down_recv, side_send, side_recv,
     row_send, row_recv, col_send, col_recv, sum_send, sum_recv,
@@ -90,8 +97,8 @@
                 )
     key_up, key_down, key_side = {}, {}, {}
     for hop in range(1, reach + 1):
-        for table, way in ((key_up, -1), (key_down, 1)):
-            table[hop] = remote(
+        for copies, way in ((key_up, -1), (key_down, 1)):
+            copies[hop] = remote(
                 keys.at[reach + way * (hop - 1), sub], keys.at[reach + way * hop, sub],
                 key_send.at[reach + way * hop, 0], key_recv.at[reach + way * hop, 0], -way, 0,
             )
@@ -152,15 +159,20 @@
     def row_of(back):
         return jnp.max(best_row[back].T, axis=0, keepdims=True)
 
-    pairs = [(d // 2, d - d // 2) for d in range(min(2 * reach, n // 2) + 1)]
-    last_row = {b: max(i for i, p in enumerate(pairs) if p[0] == b) for b in {p[0] for p in pairs}}
-    last_col = {a: max(i for i, p in enumerate(pairs) if p[1] == a) for a in {p[1] for p in pairs}}
+    pairs, last_row, last_col, late_rows, late_cols = plan(n, reach)
+    row_slot = {back: 1 + i for i, back in enumerate(late_rows)}
+    col_slot = {
+        (ahead, s): 1 + len(late_rows) + i * subs + s
+        for i, ahead in enumerate(late_cols) for s in range(subs)
+    }
     row_copies, col_copies = [], []
 
     def run(i):
         back, ahead = pairs[i]
         compare(back, ahead)
-        if back and last_row[back] == i:
+        if back in late_rows and last_row[back] == i:
+            table[place, sub, row_slot[back]] = row_of(back)
+        elif back and last_row[back] == i:
             row_out[back - 1] = row_of(back)
             copy = remote(
                 row_out.at[back - 1], row_in.at[back - 1],
@@ -168,7 +180,10 @@
             )
             copy.start()
             row_copies.append(copy)
-        if ahead and last_col[ahead] == i:
+        if ahead in late_cols and last_col[ahead] == i:
+            for s in range(subs):
+                table[place, sub, col_slot[ahead, s]] = best_col[ahead][:, s * rows : (s + 1) * rows]
+        elif ahead and last_col[ahead] == i:
             for s in range(subs):
                 col_out[ahead - 1, s] = best_col[ahead][:, s * rows : (s + 1) * rows]
             for s in range(subs):
@@ -182,7 +197,14 @@
 
     run(0)
     done = 1
+    rounds = n // 2
     for hop in range(1, reach + 1):
+        for r in range(rounds * (hop - 1) // reach, rounds * hop // reach):
+            for o, s in near:
+                pl.semaphore_signal(
+                    ready.at[r], inc=1, device_id=device(o, s), device_id_type=MESH
+                )
+            pl.semaphore_wait(ready.at[r], len(near))
         key_up[hop].wait_recv()
         key_down[hop].wait_recv()
         if hop < reach:
@@ -207,46 +229,54 @@
                 unit_right[hop, there, span(k)] = normalize(right[hop, there, span(k)])
         for s in range(1, subs):
             key_side[hop, s].wait_recv()
+        if hop == reach:
+            for copy in row_copies + col_copies:
+                copy.wait_recv()
+            base = jnp.maximum(row_of(0), floor)
+            for back in last_row:
+                if back and back not in late_rows:
+                    base = jnp.maximum(base, row_in[back - 1])
+            for ahead in last_col:
+                if ahead and ahead not in late_cols:
+                    for s in range(subs):
+                        base = jnp.maximum(base, col_in[ahead - 1, s])
+            table[place, sub, 0] = base
         while done < len(pairs) and max(pairs[done]) <= hop:
             run(done)
             done += 1
 
-    for copy in row_copies + col_copies:
-        copy.wait_recv()
-    best = jnp.maximum(row_of(0), floor)
-    for back in last_row:
-        if back:
-            best = jnp.maximum(best, row_in[back - 1])
-    for ahead in last_col:
-        if ahead:
-            for s in range(subs):
-                best = jnp.maximum(best, col_in[ahead - 1, s])
-    best_ref[...] = best
-
-    scale = math.sqrt(width)
-    limit = (2.0 + 0.5 * jnp.full((1, rows), limit_ref[0], jnp.int32).astype(jnp.float32)) / scale
-    kept = jax.nn.sigmoid(2.0 * scale * (limit - best))
-    total = jnp.sum(kept, axis=1, keepdims=True)
-    sums[blk, sub] = jnp.broadcast_to(total, (1, LANES))
-    sum_copies = [
-        remote(
-            sums.at[blk, sub], sums.at[blk, sub],
-            sum_send.at[o, s], sum_recv.at[o, s], o, s,
-        )
-        for o, s in others
+    own = table.at[place, sub]
+    table_copies = [
+        remote(own, own, sum_send.at[o, s], sum_recv.at[o, s], o, s) for o, s in reversed(others)
     ]
-    for copy in sum_copies:
+    for copy in table_copies:
         copy.start()
     for copies in (up, down, side, key_up, key_down, key_side):
         for copy in copies.values():
             copy.wait_send()
     for copy in row_copies + col_copies:
         copy.wait_send()
-    for copy in sum_copies:
+    for copy in table_copies:
         copy.wait_recv()
-    everything = jnp.sum(sums[...].reshape(n * subs, LANES), axis=0, keepdims=True)
-    share_ref[...] = (everything / (n * subs * rows))[:, :1]
-    for copy in sum_copies:
+
+    for q in range(n):
+        for s in range(subs):
+            value = table[q, s, 0]
+            for back in late_rows:
+                value = jnp.maximum(value, table[(q + back) % n, s, row_slot[back]])
+            for ahead in late_cols:
+                for t in range(subs):
+                    value = jnp.maximum(value, table[(q - ahead) % n, t, col_slot[ahead, s]])
+            maxima[q * subs + s] = value
+    best_ref[...] = maxima[place * subs + sub].reshape(rows)
+    best = maxima[...].reshape(n * subs, rows)
+    scale = math.sqrt(width)
+    index = jnp.full(best.shape, limit_ref[0], jnp.int32)
+    limit = (2.0 + 0.5 * index.astype(jnp.float32)) / scale
+    kept = jax.nn.sigmoid(2.0 * scale * (limit - best))
+    total = jnp.sum(jnp.sum(kept, axis=0, keepdims=True), axis=1, keepdims=True)
+    share_ref[...] = total / (n * subs * rows)
+    for copy in table_copies:
         copy.wait_send()
 
 
@@ -256,13 +286,15 @@
     def on_device(embeddings, member_key, limit_index):
         rows, width = embeddings.shape
         reach = -(-(n // 2) // 2)
-        chunks = 4 if rows % 64 == 0 else 1
+        chunks = 3 if rows % 48 == 0 else 1
+        late_rows, late_cols = plan(n, reach)[3:]
+        slots = 1 + len(late_rows) + len(late_cols) * subs
         dma = pltpu.SemaphoreType.DMA
         raw, f32, i32 = embeddings.dtype, jnp.float32, jnp.int32
         best, share = pl.pallas_call(
             functools.partial(kernel, n, subs, reach, chunks),
             out_shape=(
-                jax.ShapeDtypeStruct((1, rows), f32),
+                jax.ShapeDtypeStruct((rows,), f32),
                 jax.ShapeDtypeStruct((1, 1), f32),
             ),
             in_specs=[
@@ -284,7 +316,9 @@
                 pltpu.VMEM((reach, 1, rows), f32),
                 pltpu.VMEM((reach, subs, 1, rows), f32),
                 pltpu.VMEM((reach, subs, 1, rows), f32),
-                pltpu.VMEM((n, subs, 1, LANES), f32),
+                pltpu.VMEM((n, subs, slots, 1, rows), f32),
+                pltpu.VMEM((n * subs, 1, rows), f32),
+                pltpu.SemaphoreType.REGULAR((n // 2,)),
                 dma((2,)),
                 dma((2 * reach + 1, subs)),
                 dma((2 * reach + 1, subs)),
@@ -306,7 +340,7 @@
                 has_side_effects=True,
             ),
         )(embeddings, member_key.reshape(1, rows), limit_index)
-        return best.reshape(rows), share.reshape(1)
+        return best, share.reshape(1)
 
     in_specs = (P(("groups", "blk", "sub"), None), P(("groups", "blk", "sub")), P("groups"))
     out_specs = (P(("groups", "blk", "sub")), P("groups"))

time: 38.8 us -> 35.5 us (0.915)
  Pallas kernels: 34.4 us -> 31 us
    pallas_call x1, Pallas kernels: 34.4 us -> 31 us  [on_device(): pl.pallas_call(functools.partial(kernel, n, subs, reach, chunks), out_sha...]
where the time goes in v3:
time: 35.5 us; the launch traced here: 35.3 us
  Pallas kernels  31 us (87%)
  between operations  3.05 us (9%)
  local copies, waits for them, and re-layouts  1.21 us (3%)
    pallas_call x1, Pallas kernels, on_device(): pl.pallas_call(functools.partial(kernel, n, subs, reach, chunks), out_sha...  31 us
    unnamed x3, local copies, waits for them, and re-layouts  1.21 us

profile of v3, /device:TPU:0, one launch (start us, length us, event | category | flops | bytes accessed | tf_op | source)
XLA Modules:
  0.0 35.3 jit_solution(9739181100545325418)
XLA Ops:
  1.3 31.0 %shard_map.50 = (f32[192]{0:T(256)}, f32[1,1]{1,0:T(1,128)}) custom-call(bf16[192,1024]{1,0:T(8,128)(2,1)} %x_hbm.1, s32[1,192]{1,0:T(1,128)} %bitcast.2, s32[1]{0:T(128)S(6)} %copy.7.limit_ref), custom_call_target="tpu_custom_call" | custom-call | tf_op jit(solution)/shard_map/pallas_call | solution.py:294
  32.3 0.0 copy-start
  32.3 0.6 %copy-done = f32[192]{0:T(256)S(1)} copy-done((f32[192]{0:T(256)S(1)}, f32[192]{0:T(256)}, u32[]{:S(2)}) %copy-start) | copy-done | bytes 792
  33.0 0.6 %copy.8 = f32[192]{0:T(256)} copy(f32[192]{0:T(256)S(1)} %copy-done) | data formatting | bytes 1536
Async XLA Ops:
  32.3 0.7 %copy-start = (f32[192]{0:T(256)S(1)}, f32[192]{0:T(256)}, u32[]{:S(2)}) copy-start(f32[192]{0:T(256)} %get-tuple-element.8) | copy-start | bytes 2308
